TPU v7x, 32 devices: a whole 2x2x4 slice. The times are simulated.
32 devices in a mesh: dp: 2 (over x), lon: 4 (over z), lat: 4 (over y, core).
Axes of the slice: x: 2, y: 2, z: 4, core: 2. Of those that a mesh axis runs over, the one named last changes fastest.
Arguments:
- grid_in: bfloat16 [32, 64, 64, 474], P('dp', 'lat', 'lon'), parts along dimension 0
- mesh_in: bfloat16 [128, 3], P(('lat', 'lon'))
- edge_in: bfloat16 [128, 48, 4], P(('lat', 'lon'))
- senders: int32 [128, 48], P(('lat', 'lon'))
- edge_mask: int32 [128, 48], P(('lat', 'lon'))
- w_grid: bfloat16 [474, 512], replicated
- w_mesh: bfloat16 [3, 512], replicated
- w_edge: bfloat16 [4, 512], replicated
- w_msg: bfloat16 [1536, 512], replicated
- w_node: bfloat16 [1024, 512], replicated
- w_gupd: bfloat16 [512, 512], replicated
- w_out: bfloat16 [6, 512, 512], replicated
- bias_gain: float32 [6, 4, 512], replicated
Outputs:
- output 1: bfloat16 [32, 128, 512], P('dp', ('lat', 'lon')), parts along dimension 0
- output 2: bfloat16 [32, 64, 64, 512], P('dp', 'lat', 'lon'), parts along dimension 0
There are 2 independent parts. A program takes and returns all parts, laid end to end along the dimension named above; an argument that names none is the same for every part.
All inputs are finite; a program needn't handle non-finite values.
Results may differ from a plain program's by a relative error of at most 0.00871152.
Values are sent between devices in bfloat16 or wider.
A program may use at most 1 GiB of HBM per device.

v0:
```python
import functools

import jax
import jax.numpy as jnp
from jax import lax
from jax.experimental import pallas as pl
from jax.experimental.pallas import tpu as pltpu
from jax.sharding import PartitionSpec as P

REACH = 3
LN_EPS = 1e-5
FEATS = 16
TILE = 32
SUB = 256
EDGE_VMEM = 20 * 2 ** 20
NODE_VMEM = 6 * 2 ** 20
GRID_VMEM = 24 * 2 ** 20
UPDATE_VMEM = 10 * 2 ** 20
F32 = jnp.float32
BF16 = jnp.bfloat16


def mm(a, b):
    return jnp.dot(a, b, preferred_element_type=F32)


def mm_nt(a, b):
    return lax.dot_general(a, b, (((1,), (1,)), ((), ())), preferred_element_type=F32)


def gate(t):
    return (t + t * jnp.tanh(t)).astype(BF16)


def swish(x):
    return gate(x * 0.5)


def norm(y):
    scale = 1.0 / y.shape[-1]
    centered = y - jnp.sum(y, axis=-1, keepdims=True) * scale
    var = jnp.sum(centered * centered, axis=-1, keepdims=True) * scale
    return centered * lax.rsqrt(var + LN_EPS)


def mlp_tail(pre, w2, bg):
    y = mm(swish(pre), w2) + bg[1:2]
    return norm(y) * bg[2:3] + bg[3:4]


def swap_rows(value, scr, inner, put):
    outer = value.shape[0] // inner
    pitch = scr.shape[1] // outer
    for k in range(scr.shape[0]):
        for b in range(outer):
            scr[k, pl.ds(b * pitch, inner), :] = value[b * inner:(b + 1) * inner, 128 * k:128 * (k + 1)]
    for c in range(inner):
        for k in range(scr.shape[0]):
            put(c, k, scr[k, pl.ds(c, outer, stride=pitch), :].astype(BF16))


def pack_slots(send_ref, mask_ref, edge_ref, mesh_ref, lanes, table, lon, grid_cols):
    nodes, per_node = send_ref.shape
    bits = grid_cols.bit_length() - 1
    send = send_ref[...]
    row = lax.shift_right_logical(send, bits).astype(F32)
    col = (send & (grid_cols - 1)).astype(F32)
    mask = mask_ref[...].astype(F32)
    mesh = mesh_ref[...].astype(F32)
    pieces = []
    for n in range(nodes):
        here = slice(n, n + 1)
        lanes[...] = jnp.zeros_like(lanes)
        lanes[0:4, 0:per_node] = edge_ref[n].astype(F32)
        lanes[4:5, 0:per_node] = row[here]
        lanes[5:6, 0:per_node] = col[here]
        lanes[6:7, 0:per_node] = mask[here]
        lanes[7:8, 0:per_node] = jnp.full((1, per_node), n, F32) + (lon * nodes).astype(F32)
        lanes[8:11, 0:per_node] = jnp.broadcast_to(mesh[:, here], (3, per_node))
        pieces.append(lanes[...])
    for p in range(nodes // 2):
        table[:, 128 * p:128 * (p + 1)] = pieces[p] + pltpu.roll(pieces[p + nodes // 2], 64, 1)


def embed_kernel(x_ref, wg_ref, w0_ref, bg_ref, send_ref, mask_ref, edge_ref, mesh_ref,
                 vg_ref, tab_ref, band_ref,
                 scr, half, lanes, table, feat_ref, up_buf, down_buf, from_south, from_north, feat_in, up_sems, down_sems, feat_send, feat_recv, *, lats, lons):
    batch, grid_rows, cols, chans = x_ref.shape
    latent = vg_ref.shape[-1]
    step = pl.program_id(0)
    last = pl.num_programs(0) - 1
    block = scr.shape[0]
    base = lax.rem(step * last, last + 1) * block

    lat = lax.axis_index('lat')
    lon = lax.axis_index('lon')
    mesh_id = pl.DeviceIdType.MESH

    def strip(src, dst, sems, to):
        return pltpu.make_async_remote_copy(src, dst, sems.at[0], sems.at[1], device_id={'lat': to}, device_id_type=mesh_id)

    north_send = strip(up_buf, from_south, up_sems, lat - 1)
    south_send = strip(down_buf, from_north, down_sems, lat + 1)
    feats = [pltpu.make_async_remote_copy(
        feat_ref, feat_in.at[lon], feat_send.at[k - 1], feat_recv.at[k - 1],
        device_id={'lon': lax.rem(lon + k, lons)}, device_id_type=mesh_id) for k in range(1, lons)]

    @pl.when(step == 0)
    def _():
        barrier = pltpu.get_barrier_semaphore()
        for k in range(1, lons):
            pl.semaphore_signal(barrier, 1, device_id={'lon': lax.rem(lon + k, lons)}, device_id_type=mesh_id)

        @pl.when(lat > 0)
        def _():
            pl.semaphore_signal(barrier, 1, device_id={'lat': lat - 1}, device_id_type=mesh_id)

        @pl.when(lat < lats - 1)
        def _():
            pl.semaphore_signal(barrier, 1, device_id={'lat': lat + 1}, device_id_type=mesh_id)

        pack_slots(send_ref, mask_ref, edge_ref, mesh_ref, lanes, table, lon, cols * lons)
        feat_ref[...] = table[...].astype(BF16)

    @pl.when(step == 1)
    def _():
        barrier = pltpu.get_barrier_semaphore()
        inner = (lat > 0).astype(jnp.int32) + (lat < lats - 1).astype(jnp.int32)
        pl.semaphore_wait(barrier, lons - 1 + inner)

        @pl.when(lat > 0)
        def _():
            north_send.start()

        feat_in[lon] = feat_ref[...]
        for copy in feats:
            copy.start()

    @pl.when((step == 2) & (lat < lats - 1))
    def _():
        south_send.start()

    rows = batch * cols
    halve(half, wg_ref)
    bg = bg_ref[0]
    b1 = bg[0:1] * 0.5

    def first(r):
        return gate(mm(x_ref[:, base + r].reshape(rows, chans), half[...]) + b1)

    def second(r, hid):
        vg = norm(mm(hid, w0_ref[0]) + bg[1:2]) * bg[2:3] + bg[3:4]
        vg_ref[:, base + r] = vg.astype(BF16).reshape(batch, cols, latent)

        def put(c, k, part):
            tab_ref[REACH + base + r, c, :, 128 * k:128 * (k + 1)] = part

        swap_rows(vg, scr.at[r], cols, put)

    staged(block, first, second)

    @pl.when(step == 0)
    def _():
        up_buf[...] = tab_ref[REACH:2 * REACH]

    @pl.when(step == 1)
    def _():
        down_buf[...] = tab_ref[grid_rows:grid_rows + REACH]

    @pl.when(step == last)
    def _():
        for copy in feats:
            copy.wait()
        band_ref[...] = feat_in[...]

        @pl.when(lat > 0)
        def _():
            north_send.wait_send()
            south_send.wait_recv()
            tab_ref[0:REACH] = from_north[...]

        @pl.when(lat < lats - 1)
        def _():
            south_send.wait_send()
            north_send.wait_recv()
            tab_ref[grid_rows + REACH:grid_rows + 2 * REACH] = from_south[...]


def embed_call(grid_in, w_grid, w_out, bias_gain, senders, edge_mask, edge_t, mesh_t, lats, lons, block):
    batch, rows, cols, chans = grid_in.shape
    latent = w_out.shape[-1]
    steps = rows // block
    nodes = senders.shape[0]
    feats = jax.ShapeDtypeStruct((FEATS, nodes // 2 * 128), BF16)
    whole = lambda *shape: pl.BlockSpec(shape, lambda r: (0,) * len(shape))
    pick = lambda k, *shape: pl.BlockSpec((1,) + shape, lambda r: (k,) + (0,) * len(shape))
    strip = (REACH, cols, batch, latent)
    local = pl.BlockSpec(memory_space=pltpu.VMEM)
    return pl.pallas_call(
        functools.partial(embed_kernel, lats=lats, lons=lons),
        grid=(steps,),
        in_specs=[
            local,
            whole(chans, latent), pick(0, latent, latent), pick(0, 4, latent), whole(*senders.shape),
            whole(*edge_mask.shape), whole(*edge_t.shape), whole(*mesh_t.shape)],
        out_specs=[local, local, local],
        out_shape=[
            jax.ShapeDtypeStruct((batch, rows, cols, latent), BF16),
            jax.ShapeDtypeStruct((rows + 2 * REACH, cols, batch, latent), BF16),
            jax.ShapeDtypeStruct((lons,) + feats.shape, BF16)],
        scratch_shapes=[
            pltpu.VMEM((block, latent // 128, batch * (cols + 8), 128), F32),
            pltpu.VMEM((chans, latent), BF16), pltpu.VMEM((FEATS, 128), F32), pltpu.VMEM(feats.shape, F32),
            pltpu.VMEM(feats.shape, BF16),
            pltpu.VMEM(strip, BF16), pltpu.VMEM(strip, BF16), pltpu.VMEM(strip, BF16), pltpu.VMEM(strip, BF16),
            pltpu.VMEM((lons,) + feats.shape, BF16),
            pltpu.SemaphoreType.DMA((2,)), pltpu.SemaphoreType.DMA((2,)),
            pltpu.SemaphoreType.DMA((lons - 1,)), pltpu.SemaphoreType.DMA((lons - 1,))],
        compiler_params=pltpu.CompilerParams(collective_id=0, has_side_effects=True, vmem_limit_bytes=GRID_VMEM),
        cost_estimate=pl.CostEstimate(
            flops=4 * rows * batch * cols * latent * latent, transcendentals=0,
            bytes_accessed=6 * rows * batch * cols * latent),
        name='embed',
    )(grid_in, w_grid, w_out, bias_gain, senders, edge_mask, edge_t, mesh_t)


def halve(dst, src):
    @pl.when(pl.program_id(0) == 0)
    def _():
        dst[...] = src[...] * jnp.asarray(0.5, BF16)


def staged(count, first, second):
    hid = first(0)
    for i in range(count):
        nxt = first(i + 1) if i + 1 < count else None
        second(i, hid)
        hid = nxt


def update_kernel(vg_ref, wu_ref, w5_ref, bg_ref, dep_ref, out_ref, half):
    halve(half, wu_ref)
    bg = bg_ref[0]
    b1 = bg[0:1] * 0.5
    base = pl.program_id(0) * out_ref.shape[0]

    def rows(i):
        return pl.ds(pl.multiple_of(base + i * SUB, SUB), SUB)

    def first(i):
        return gate(mm(vg_ref[rows(i), :], half[...]) + b1)

    def second(i, hid):
        upd = norm(mm(hid, w5_ref[0]) + bg[1:2]) * bg[2:3] + bg[3:4]
        out_ref[i * SUB:(i + 1) * SUB] = (vg_ref[rows(i), :].astype(F32) + upd).astype(BF16)

    staged(out_ref.shape[0] // SUB, first, second)


def update_call(vg, w_gupd, w_out, bias_gain, dep, block):
    rows, latent = vg.shape
    pick = lambda k, *shape: pl.BlockSpec((1,) + shape, lambda r: (k,) + (0,) * len(shape))
    tile = pl.BlockSpec((block, latent), lambda r: (r, 0))
    return pl.pallas_call(
        update_kernel,
        grid=(rows // block,),
        in_specs=[pl.BlockSpec(memory_space=pltpu.VMEM), pl.BlockSpec((latent, latent), lambda r: (0, 0)), pick(5, latent, latent), pick(5, 4, latent),
                  pl.BlockSpec(memory_space=pl.ANY)],
        out_specs=tile,
        out_shape=jax.ShapeDtypeStruct(vg.shape, BF16),
        scratch_shapes=[pltpu.VMEM((latent, latent), BF16)],
        cost_estimate=pl.CostEstimate(flops=4 * rows * latent * latent, transcendentals=0, bytes_accessed=4 * rows * latent),
        compiler_params=pltpu.CompilerParams(vmem_limit_bytes=UPDATE_VMEM),
        name='update',
    )(vg, w_gupd, w_out, bias_gain, dep)


def edge_kernel(v_ref, we_ref, wm_ref, wmsg_ref, wo_ref, wn_ref, bg_ref,
                tab_ref, *rest, lats, lons, near):
    lp, ec, vmf, idx_v, idx_s, part, half, hid_a, hid_b, xbuf, isem = rest[-11:]
    outs = rest[:-11]
    latent = wo_ref.shape[-1]
    slots = lons * v_ref.shape[-1]
    grid_rows, cols, batch = tab_ref.shape[:3]
    positions = grid_rows * cols
    cell_rows = grid_rows - 2 * REACH
    table = tab_ref.reshape(positions, batch, latent)
    nodes = outs[0].shape[0]
    band = lons * nodes
    lat = lax.axis_index('lat')
    lon = lax.axis_index('lon')
    vtb = jnp.concatenate([v_ref[k] for k in range(lons)], axis=1)
    vt = vtb.astype(F32)
    ids = lax.broadcasted_iota(jnp.int32, (band, slots), 0)
    local = lax.rem(ids, nodes)
    pick_row = lax.div(ids, nodes) * (slots // lons) + lax.rem(local, nodes // 2) * 128 + lax.div(local, nodes // 2) * 64
    pick = lax.broadcasted_iota(jnp.int32, (band, slots), 1) == pick_row
    mesh_feat = mm_nt(jnp.where(pick, 1.0, 0.0).astype(BF16), vtb).astype(BF16)
    we = jnp.concatenate([we_ref[...].astype(F32), jnp.zeros((FEATS - 4, latent), F32)], axis=0).astype(BF16)
    wm = jnp.concatenate(
        [jnp.zeros((8, latent), F32), wm_ref[...].astype(F32), jnp.zeros((FEATS - 11, latent), F32)], axis=0).astype(BF16)
    bg1 = bg_ref[1]
    bg2 = bg_ref[2]
    bg3 = bg_ref[3]
    vm = mlp_tail(mm(mesh_feat, wm) + bg1[0:1], wo_ref[1], bg1).astype(BF16)
    if near:
        vmf[...] = vm.astype(F32)
        own_vm = vmf[pl.ds(pl.multiple_of(lon * nodes, 8), nodes), :]
        outs[1][...] = own_vm
        outs[2][...] = mm(own_vm.astype(BF16), wn_ref[0:latent, :]) + bg_ref[4][0:1]

    col = vt[5:6] - (lon * cols).astype(F32)
    cell = vt[7:8] - (lon * nodes).astype(F32)
    inner = (cell > -0.5) & (cell < nodes - 0.5)
    wanted = inner if near else jnp.logical_not(inner)
    flag = jnp.where((vt[6:7] > 0.5) & (col > -0.5) & (col < cols - 0.5) & wanted, 1.0, 0.0)
    chunks = slots // 128
    pad = -chunks % 16
    rows = [flag[:, 128 * c:128 * (c + 1)] for c in range(chunks)] + [jnp.zeros((pad, 128), F32)] * (pad > 0)
    flags = jnp.concatenate(rows, axis=0)
    up = lax.broadcasted_iota(jnp.int32, (128, 128), 0) <= lax.broadcasted_iota(jnp.int32, (128, 128), 1)
    incl = mm(flags.astype(BF16), jnp.where(up, 1.0, 0.0).astype(BF16))
    n_rows = chunks + pad
    low = lax.broadcasted_iota(jnp.int32, (n_rows, n_rows), 1) < lax.broadcasted_iota(jnp.int32, (n_rows, n_rows), 0)
    row_sum = jnp.broadcast_to(incl[:, 127:128], (n_rows, 128)).astype(BF16)
    before = mm(jnp.where(low, 1.0, 0.0).astype(BF16), row_sum)
    rank = jnp.where(flags > 0.5, incl + before - 1.0, -1.0)
    total = jnp.sum(flag).astype(jnp.int32)

    def prep(t, carry):
        slot = (lax.broadcasted_iota(jnp.int32, (128, 128), 0) + t * 128).astype(F32)
        sel = jnp.concatenate(
            [jnp.where(rank[c:c + 1] == slot, 1.0, 0.0).astype(BF16) for c in range(chunks)], axis=1)
        feat = mm_nt(sel, vtb).astype(BF16)
        feat_t = mm_nt(vtb, sel)
        here = pl.ds(pl.multiple_of(t * 128, 128), 128)
        live = lax.broadcasted_iota(jnp.int32, (1, 128), 1) + t * 128 < total
        win_r = feat_t[4:5] - (lat * cell_rows - REACH).astype(F32)
        win_c = feat_t[5:6] - (lon * cols).astype(F32)
        pos = jnp.where(live, (win_r * cols + win_c).astype(jnp.int32), REACH * cols)
        node = feat_t[7:8].astype(jnp.int32)
        rel = lax.rem(node + (lons - lon) * nodes, band)
        idx_v[0:1, here] = jnp.clip(pos, 0, positions - 1)
        idx_v[1:2, here] = jnp.where(live, rel, band)
        edge = mlp_tail(mm(feat, we) + bg2[0:1], wo_ref[2], bg2).astype(BF16)
        node_col = feat[:, 7:8].astype(F32)
        hot = lax.broadcasted_iota(jnp.int32, (128, band), 1).astype(F32) == node_col
        vm_e = mm(jnp.where(hot, 1.0, 0.0).astype(BF16), vm).astype(BF16)
        lp[here, :] = (mm(edge, wmsg_ref[0:latent, :]) + mm(vm_e, wmsg_ref[2 * latent:, :]) + bg3[0:1]) * 0.5
        ec[here, :] = edge.astype(F32) + bg3[3:4]
        return carry

    lax.fori_loop(0, lax.div(total + 127, 128), prep, 0)
    move = pltpu.make_async_copy(idx_v, idx_s, isem)
    move.start()
    part[...] = jnp.zeros_like(part)
    half[...] = wmsg_ref[latent:2 * latent, :] * jnp.asarray(0.5, BF16)
    move.wait()

    per = TILE // 2
    bufs = (xbuf.at[0], xbuf.at[1])
    hids = (hid_a, hid_b)

    def first(base, k):
        for s in range(per):
            bufs[k][pl.ds(s * batch, batch), :] = table[idx_s[0, base + s]]
        acc = mm(bufs[k][...], half[...]).reshape(per, batch, latent)
        here = pl.ds(pl.multiple_of(base, per), per)
        hids[k][...] = gate(acc + lp[here, :].reshape(per, 1, latent)).reshape(per * batch, latent)

    def second(base, k):
        y = mm(hids[k][...], wo_ref[3]) + bg3[1:2]
        here = pl.ds(pl.multiple_of(base, per), per)
        z = (norm(y) * bg3[2:3]).reshape(per, batch, latent) + ec[here, :].reshape(per, 1, latent)
        z = z.astype(BF16).astype(F32)
        for s in range(per):
            n = idx_s[1, base + s]
            part[n] += z[s]

    tiles = lax.div(total + TILE - 1, TILE)

    @pl.when(tiles > 0)
    def _():
        first(0, 0)

    def edges(t, carry):
        base = t * TILE
        first(base + per, 1)
        second(base, 0)
        first(jnp.minimum(t + 1, tiles - 1) * TILE, 0)
        second(base + per, 1)
        return carry

    lax.fori_loop(0, tiles, edges, 0)
    if near:
        outs[0][...] = part[0:nodes]
    else:
        for k in range(1, lons):
            outs[k - 1][...] = part[k * nodes:(k + 1) * nodes]


def edge_call(v, w_edge, w_mesh, w_msg, w_out, w_node, bias_gain, table, lats, lons, nodes, per_node, near):
    latent = w_out.shape[-1]
    slots = lons * v.shape[-1]
    batch = table.shape[2]
    whole = lambda a: pl.BlockSpec(a.shape, lambda r: (0,) * a.ndim)
    pick = lambda k, *shape: pl.BlockSpec((1,) + shape, lambda r: (k,) + (0,) * len(shape))
    limit = lons * nodes * per_node
    block = jax.ShapeDtypeStruct((nodes, batch, latent), F32)
    row = jax.ShapeDtypeStruct((nodes, latent), F32)
    outs = [block] + [row] * 2 if near else [block] * (lons - 1)
    local = pl.BlockSpec(memory_space=pltpu.VMEM)
    return pl.pallas_call(
        functools.partial(edge_kernel, lats=lats, lons=lons, near=near),
        in_specs=[local] * 8,
        out_specs=[local] * len(outs),
        out_shape=outs,
        scratch_shapes=[
            pltpu.VMEM((limit, latent), F32),
            pltpu.VMEM((limit, latent), F32),
            pltpu.VMEM((lons * nodes, latent), F32),
            pltpu.VMEM((8, limit), jnp.int32),
            pltpu.SMEM((8, limit), jnp.int32),
            pltpu.VMEM((lons * nodes + 1, batch, latent), F32),
            pltpu.VMEM((latent, latent), BF16),
            pltpu.VMEM((TILE // 2 * batch, latent), BF16),
            pltpu.VMEM((TILE // 2 * batch, latent), BF16),
            pltpu.VMEM((2, TILE // 2 * batch, latent), BF16),
            pltpu.SemaphoreType.DMA],
        cost_estimate=pl.CostEstimate(
            flops=4 * slots // 4 * batch * latent * latent, transcendentals=0, bytes_accessed=2 * slots * batch * latent),
        compiler_params=pltpu.CompilerParams(vmem_limit_bytes=EDGE_VMEM),
        name='edges_near' if near else 'edges_far',
    )(v, w_edge, w_mesh, w_msg, w_out, w_node, bias_gain, table)


def node_kernel(own_ref, r1_ref, r2_ref, r3_ref, vm_ref, nb_ref, wn_ref, w4_ref, bg_ref, out_ref, scr):
    nodes, batch, latent = own_ref.shape
    agg = (own_ref[...] + r1_ref[...] + r2_ref[...] + r3_ref[...]).astype(BF16).reshape(nodes * batch, latent)
    acc = mm(agg, wn_ref[latent:, :]).reshape(nodes, batch, latent) + nb_ref[...].reshape(nodes, 1, latent)
    bg = bg_ref[4]
    upd = mlp_tail(acc.reshape(nodes * batch, latent), w4_ref[4], bg)
    out = (upd.reshape(nodes, batch, latent) + vm_ref[...].reshape(nodes, 1, latent)).reshape(nodes * batch, latent)

    def put(b, k, part):
        out_ref[b, :, 128 * k:128 * (k + 1)] = part

    swap_rows(out, scr, batch, put)


def node_call(blocks, vm, nb, w_node, w_out, bias_gain):
    nodes, batch, latent = blocks[0].shape
    local = pl.BlockSpec(memory_space=pltpu.VMEM)
    out = jax.ShapeDtypeStruct((batch, nodes, latent), BF16)
    return pl.pallas_call(
        node_kernel,
        in_specs=[local] * 9,
        out_specs=local,
        out_shape=out,
        compiler_params=pltpu.CompilerParams(vmem_limit_bytes=NODE_VMEM),
        scratch_shapes=[pltpu.VMEM((latent // 128, nodes * (batch + 8), 128), F32)],
        name='nodes',
    )(*blocks, vm, nb, w_node, w_out, bias_gain)


def solution(mesh):
    lats = mesh.shape['lat']
    lons = mesh.shape['lon']
    south_shift = [(s, s + 1) for s in range(lats - 1)]
    north_shift = [(s + 1, s) for s in range(lats - 1)]

    def cell_step(grid_in, mesh_in, edge_in, senders, edge_mask, w_grid, w_mesh, w_edge, w_msg, w_node, w_gupd, w_out, bias_gain):
        batch, rows, cols, _ = grid_in.shape
        nodes = senders.shape[0]
        latent = w_out.shape[-1]
        vg, table, band = embed_call(
            grid_in, w_grid, w_out, bias_gain, senders, edge_mask, jnp.swapaxes(edge_in, 1, 2), mesh_in.T, lats, lons, 4)
        edges = functools.partial(
            edge_call, band, w_edge, w_mesh, w_msg, w_out, w_node, bias_gain, table, lats, lons, *senders.shape)
        p1, p2, p3 = edges(False)
        own, vm, nb = edges(True)
        pairs = lambda k, polar: [
            (j * lats + i, (j + k) % lons * lats + i) for i in range(lats) for j in range(lons)
            if not polar or i in (0, lats - 1)]
        got = [lax.ppermute(p, ('lon', 'lat'), pairs(k, 1 < k < lons - 1)) for k, p in ((2, p2), (1, p1), (3, p3))]
        flat = update_call(vg.reshape(batch * rows * cols, latent), w_gupd, w_out, bias_gain, nb, 1024)
        grid_out = flat.reshape(batch, rows, cols, latent)
        mesh_out = node_call([own] + got, vm, nb, w_node, w_out, bias_gain)
        return mesh_out, grid_out

    grid_spec = P('dp', 'lat', 'lon', None)
    node_spec = P(('lat', 'lon'), None)
    slot_spec = P(('lat', 'lon'), None, None)
    in_specs = (grid_spec, node_spec, slot_spec, node_spec, node_spec) + (P(),) * 8
    out_specs = (P('dp', ('lat', 'lon'), None), grid_spec)
    return jax.shard_map(cell_step, mesh=mesh, in_specs=in_specs, out_specs=out_specs, check_vma=False)
```

profile of v0, /device:TPU:0, one launch (start us, length us, event | category | flops | bytes accessed | tf_op | source)
XLA Modules:
  0.0 59.5 jit_solution(16260791959558897819)
XLA Ops:
  0.6 0.0 copy-start
  0.6 1.9 %copy-done = bf16[6,512,512]{2,1,0:T(8,128)(2,1)S(1)} copy-done((bf16[6,512,512]{2,1,0:T(8,128)(2,1)S(1)}, bf16[6,512,512]{2,1,0:T(8,128)(2,1)}, u32[]{:S(2)}) %copy-start) | copy-done | bytes 3145752
  2.5 0.0 copy-start.3
  2.5 0.8 %copy-done.3 = f32[6,4,512]{2,1,0:T(4,128)S(1)} copy-done((f32[6,4,512]{2,1,0:T(4,128)S(1)}, f32[6,4,512]{2,1,0:T(4,128)}, u32[]{:S(2)}) %copy-start.3) | copy-done | bytes 49176
  3.3 0.0 copy-start.5
  3.3 2.2 %copy-done.5 = bf16[16,16,16,474]{3,2,1,0:T(8,128)(2,1)S(1)} copy-done((bf16[16,16,16,474]{3,2,1,0:T(8,128)(2,1)S(1)}, bf16[16,16,16,474]{3,2,1,0:T(8,128)(2,1)}, u32[]{:S(2)}) %copy-start.5) | copy-done | bytes 3883032
  5.5 0.0 copy-start.8
  5.5 1.0 %copy-done.8 = bf16[474,512]{1,0:T(8,128)(2,1)S(1)} copy-done((bf16[474,512]{1,0:T(8,128)(2,1)S(1)}, bf16[474,512]{1,0:T(8,128)(2,1)}, u32[]{:S(2)}) %copy-start.8) | copy-done | bytes 485400
  6.5 0.0 copy-start.9
  6.5 0.7 %copy-done.9 = bf16[8,48,4]{1,2,0:T(4,128)(2,1)S(1)} copy-done((bf16[8,48,4]{1,2,0:T(4,128)(2,1)S(1)}, bf16[8,48,4]{1,2,0:T(4,128)(2,1)}, u32[]{:S(2)}) %copy-start.9) | copy-done | bytes 3096
  7.2 0.0 copy-start.10
  7.2 0.7 %copy-done.10 = s32[8,48]{1,0:T(8,128)S(1)} copy-done((s32[8,48]{1,0:T(8,128)S(1)}, s32[8,48]{1,0:T(8,128)}, u32[]{:S(2)}) %copy-start.10) | copy-done | bytes 1560
  7.9 0.0 copy-start.11
  7.9 0.7 %copy-done.11 = s32[8,48]{1,0:T(8,128)S(1)} copy-done((s32[8,48]{1,0:T(8,128)S(1)}, s32[8,48]{1,0:T(8,128)}, u32[]{:S(2)}) %copy-start.11) | copy-done | bytes 1560
  8.6 0.0 copy-start.14
  8.6 0.7 %copy-done.14 = bf16[8,3]{0,1:T(4,128)(2,1)S(1)} copy-done((bf16[8,3]{0,1:T(4,128)(2,1)S(1)}, bf16[8,3]{0,1:T(4,128)(2,1)}, u32[]{:S(2)}) %copy-start.14) | copy-done | bytes 72
  9.3 0.0 copy-start.1
  9.3 0.0 copy-start.2
  9.3 0.0 copy-start.4
  9.3 0.0 copy-start.6
  9.3 0.0 copy-start.12
  9.3 0.0 copy-start.13
  9.3 11.6 %embed.1 = (bf16[16,16,16,512]{3,2,1,0:T(8,128)(2,1)S(1)}, bf16[22,16,16,512]{3,2,1,0:T(8,128)(2,1)S(1)}, bf16[4,16,512]{2,1,0:T(8,128)(2,1)S(1)}) custom-call(bf16[16,16,16,474]{3,2,1,0:T(8,128)(2,1)S(1)} %copy-done.5, bf16[474,512]{1,0:T(8,128)(2,1)S(1)} %copy-done.8, bf16[6,512,512]{2,1,0:T(8,128)(2,1)S(1)} %copy-done, f32[6,4,512]{2,1,0:T(4,128)S(1)} %copy-done.3, ...), custom_call_target="tpu_custom_call" | custom-call | flops 4294967296 | bytes 12582912 | tf_op jit(solution)/shard_map/embed/pallas_call | solution.py:199
  20.9 0.0 copy-done.1
  20.9 0.0 copy-done.2
  21.0 0.0 copy-done.4
  21.0 0.0 copy-done.6
  21.0 0.0 copy-done.12
  21.0 0.0 copy-done.13
  21.0 7.9 %edges_far.1 = (f32[8,16,512]{2,1,0:T(8,128)S(1)}, f32[8,16,512]{2,1,0:T(8,128)S(1)}, f32[8,16,512]{2,1,0:T(8,128)S(1)}) custom-call(bf16[4,16,512]{2,1,0:T(8,128)(2,1)S(1)} %get-tuple-element.11.v_ref, bf16[4,512]{1,0:T(4,128)(2,1)S(1)} %copy-done.12, bf16[3,512]{1,0:T(4,128)(2,1)S(1)} %copy-done.13, bf16[1536,512]{1,0:T(8,128)(2,1)S(1)} %copy-done.6, ...), custom_call_target="tpu_custom_call" | custom-call | flops 8589934592 | bytes 33554432 | tf_op jit(solution)/shard_map/edges_far/pallas_call | solution.py:413
  28.9 5.5 %collective-permute-start = (f32[8,16,512]{2,1,0:T(8,128)S(1)}, f32[8,16,512]{2,1,0:T(8,128)S(1)}, u32[]{:S(2)}, u32[]{:S(2)}) collective-permute-start(f32[8,16,512]{2,1,0:T(8,128)S(1)} %get-tuple-element.14), channel_id=1, source_target_pairs={{0,8},{4,12},{8,0},{12,4},{3,11},{7,15},{11,3},{15,7},{16,24},{20,... | collective-permute-start | bytes 786440 | tf_op jit(solution)/shard_map/ppermute | solution.py:485
  34.4 0.1 collective-permute-start.1
  34.5 0.0 copy-start.7
  34.5 3.8 %collective-permute-start.2 = (f32[8,16,512]{2,1,0:T(8,128)S(1)}, f32[8,16,512]{2,1,0:T(8,128)S(1)}, u32[]{:S(2)}, u32[]{:S(2)}) collective-permute-start(f32[8,16,512]{2,1,0:T(8,128)S(1)} %get-tuple-element.16), channel_id=1, source_target_pairs={{0,12},{4,0},{8,4},{12,8},{1,13},{5,1},{9,5},{13,9},{2,14},{6,2},{... | collective-permute-start | bytes 786440 | tf_op jit(solution)/shard_map/ppermute | solution.py:485
  38.3 11.5 %edges_near.1 = (f32[8,16,512]{2,1,0:T(8,128)S(1)}, f32[8,512]{1,0:T(8,128)S(1)}, f32[8,512]{1,0:T(8,128)S(1)}) custom-call(bf16[4,16,512]{2,1,0:T(8,128)(2,1)S(1)} %get-tuple-element.11.v_ref, bf16[4,512]{1,0:T(4,128)(2,1)S(1)} %copy-done.12, bf16[3,512]{1,0:T(4,128)(2,1)S(1)} %copy-done.13, bf16[1536,512]{1,0:T(8,128)(2,1)S(1)} %copy-done.6, ...), custom_call_target="tpu_custom_call" | custom-call | flops 8589934592 | bytes 33554432 | tf_op jit(solution)/shard_map/edges_near/pallas_call | solution.py:413
  49.8 0.0 copy-done.7
  49.9 8.3 %update.1 = bf16[4096,512]{1,0:T(8,128)(2,1)} custom-call(bf16[4096,512]{1,0:T(8,128)(2,1)S(1)} %bitcast.6, bf16[512,512]{1,0:T(8,128)(2,1)S(1)} %copy-done.7, bf16[6,512,512]{2,1,0:T(8,128)(2,1)S(1)} %copy-done.1, f32[6,4,512]{2,1,0:T(4,128)S(1)} %copy-done.4, f32[8,512]{1,0:T(8,128)S(1)} %get-tuple-element.18.nb_ref.dep_ref), custom_call_target="tpu_custom_call" | custom-call | flops 4294967296 | bytes 8388608 | tf_op jit(solution)/shard_map/update/pallas_call | solution.py:264
  58.1 0.0 collective-permute-done.r1_ref
  58.1 0.0 collective-permute-done.1.r2_ref
  58.1 0.0 collective-permute-done.2.r3_ref
  58.1 1.3 %nodes.1 = bf16[16,8,512]{2,1,0:T(8,128)(2,1)} custom-call(f32[8,16,512]{2,1,0:T(8,128)S(1)} %get-tuple-element.13.own_ref, f32[8,16,512]{2,1,0:T(8,128)S(1)} %collective-permute-done.r1_ref, f32[8,16,512]{2,1,0:T(8,128)S(1)} %collective-permute-done.1.r2_ref, f32[8,16,512]{2,1,0:T(8,128)S(1)} %collective-permute-done.2.r3_ref, ...), custom_call_target="tpu_custom_call" | custom-call | tf_op jit(solution)/shard_map/nodes/pallas_call | solution.py:455
Async XLA Ops:
  0.6 1.9 %copy-start = (bf16[6,512,512]{2,1,0:T(8,128)(2,1)S(1)}, bf16[6,512,512]{2,1,0:T(8,128)(2,1)}, u32[]{:S(2)}) copy-start(bf16[6,512,512]{2,1,0:T(8,128)(2,1)} %w5_ref.1) | copy-start | bytes 9437188
  2.5 0.8 %copy-start.3 = (f32[6,4,512]{2,1,0:T(4,128)S(1)}, f32[6,4,512]{2,1,0:T(4,128)}, u32[]{:S(2)}) copy-start(f32[6,4,512]{2,1,0:T(4,128)} %bg_ref.9) | copy-start | bytes 147460
  3.3 2.2 %copy-start.5 = (bf16[16,16,16,474]{3,2,1,0:T(8,128)(2,1)S(1)}, bf16[16,16,16,474]{3,2,1,0:T(8,128)(2,1)}, u32[]{:S(2)}) copy-start(bf16[16,16,16,474]{3,2,1,0:T(8,128)(2,1)} %x_ref.1) | copy-start | bytes 11649028
  5.5 1.0 %copy-start.8 = (bf16[474,512]{1,0:T(8,128)(2,1)S(1)}, bf16[474,512]{1,0:T(8,128)(2,1)}, u32[]{:S(2)}) copy-start(bf16[474,512]{1,0:T(8,128)(2,1)} %wg_ref.1) | copy-start | bytes 1456132
  6.5 0.7 %copy-start.9 = (bf16[8,48,4]{1,2,0:T(4,128)(2,1)S(1)}, bf16[8,48,4]{1,2,0:T(4,128)(2,1)}, u32[]{:S(2)}) copy-start(bf16[8,48,4]{1,2,0:T(4,128)(2,1)} %param.15) | copy-start | bytes 9220
  7.2 0.7 %copy-start.10 = (s32[8,48]{1,0:T(8,128)S(1)}, s32[8,48]{1,0:T(8,128)}, u32[]{:S(2)}) copy-start(s32[8,48]{1,0:T(8,128)} %send_ref.1) | copy-start | bytes 4612
  7.9 0.7 %copy-start.11 = (s32[8,48]{1,0:T(8,128)S(1)}, s32[8,48]{1,0:T(8,128)}, u32[]{:S(2)}) copy-start(s32[8,48]{1,0:T(8,128)} %mask_ref.1) | copy-start | bytes 4612
  8.6 0.7 %copy-start.14 = (bf16[8,3]{0,1:T(4,128)(2,1)S(1)}, bf16[8,3]{0,1:T(4,128)(2,1)}, u32[]{:S(2)}) copy-start(bf16[8,3]{0,1:T(4,128)(2,1)} %param.14) | copy-start | bytes 148
  9.3 11.6 %copy-start.1 = (bf16[6,512,512]{2,1,0:T(8,128)(2,1)S(1)}, bf16[6,512,512]{2,1,0:T(8,128)(2,1)}, u32[]{:S(2)}) copy-start(bf16[6,512,512]{2,1,0:T(8,128)(2,1)} %w5_ref.1) | copy-start | bytes 9437188
  9.3 11.6 %copy-start.2 = (bf16[1024,512]{1,0:T(8,128)(2,1)S(1)}, bf16[1024,512]{1,0:T(8,128)(2,1)}, u32[]{:S(2)}) copy-start(bf16[1024,512]{1,0:T(8,128)(2,1)} %wn_ref.5) | copy-start | bytes 3145732
  9.3 11.7 %copy-start.4 = (f32[6,4,512]{2,1,0:T(4,128)S(1)}, f32[6,4,512]{2,1,0:T(4,128)}, u32[]{:S(2)}) copy-start(f32[6,4,512]{2,1,0:T(4,128)} %bg_ref.9) | copy-start | bytes 147460
  9.3 11.7 %copy-start.6 = (bf16[1536,512]{1,0:T(8,128)(2,1)S(1)}, bf16[1536,512]{1,0:T(8,128)(2,1)}, u32[]{:S(2)}) copy-start(bf16[1536,512]{1,0:T(8,128)(2,1)} %wmsg_ref.3) | copy-start | bytes 4718596
  9.3 11.7 %copy-start.12 = (bf16[4,512]{1,0:T(4,128)(2,1)S(1)}, bf16[4,512]{1,0:T(4,128)(2,1)}, u32[]{:S(2)}) copy-start(bf16[4,512]{1,0:T(4,128)(2,1)} %we_ref.3) | copy-start | bytes 12292
  9.3 11.7 %copy-start.13 = (bf16[3,512]{1,0:T(4,128)(2,1)S(1)}, bf16[3,512]{1,0:T(4,128)(2,1)}, u32[]{:S(2)}) copy-start(bf16[3,512]{1,0:T(4,128)(2,1)} %wm_ref.3) | copy-start | bytes 9220
  28.9 29.2 %collective-permute-start = (f32[8,16,512]{2,1,0:T(8,128)S(1)}, f32[8,16,512]{2,1,0:T(8,128)S(1)}, u32[]{:S(2)}, u32[]{:S(2)}) collective-permute-start(f32[8,16,512]{2,1,0:T(8,128)S(1)} %get-tuple-element.14), channel_id=1, source_target_pairs={{0,8},{4,12},{8,0},{12,4},{3,11},{7,15},{11,3},{15,7},{16,24},{20,... | collective-permute-start | bytes 786440 | tf_op jit(solution)/shard_map/ppermute | solution.py:485
  34.4 23.7 %collective-permute-start.1 = (f32[8,16,512]{2,1,0:T(8,128)S(1)}, f32[8,16,512]{2,1,0:T(8,128)S(1)}, u32[]{:S(2)}, u32[]{:S(2)}) collective-permute-start(f32[8,16,512]{2,1,0:T(8,128)S(1)} %get-tuple-element.15), channel_id=1, source_target_pairs={{0,4},{4,8},{8,12},{12,0},{1,5},{5,9},{9,13},{13,1},{2,6},{6,10},{... | collective-permute-start | bytes 786440 | tf_op jit(solution)/shard_map/ppermute | solution.py:485
  34.5 15.3 %copy-start.7 = (bf16[512,512]{1,0:T(8,128)(2,1)S(1)}, bf16[512,512]{1,0:T(8,128)(2,1)}, u32[]{:S(2)}) copy-start(bf16[512,512]{1,0:T(8,128)(2,1)} %wu_ref.1) | copy-start | bytes 1572868
  34.5 23.6 %collective-permute-start.2 = (f32[8,16,512]{2,1,0:T(8,128)S(1)}, f32[8,16,512]{2,1,0:T(8,128)S(1)}, u32[]{:S(2)}, u32[]{:S(2)}) collective-permute-start(f32[8,16,512]{2,1,0:T(8,128)S(1)} %get-tuple-element.16), channel_id=1, source_target_pairs={{0,12},{4,0},{8,4},{12,8},{1,13},{5,1},{9,5},{13,9},{2,14},{6,2},{... | collective-permute-start | bytes 786440 | tf_op jit(solution)/shard_map/ppermute | solution.py:485
where the time goes:
time: 58.8 us; the launch traced here: 59.5 us
  Pallas kernels  40.6 us (69%)
  starting transfers between devices  9.37 us (16%)
  local copies, waits for them, and re-layouts  8.67 us (15%)
  between operations  0.78 us (1%)
    pallas_call x2, Pallas kernels, edge_call(): pl.pallas_call(functools.partial(edge_kernel, lats=lats, lons=lons, near=...  19.4 us
    pallas_call x1, Pallas kernels, embed_call(): pl.pallas_call(functools.partial(embed_kernel, lats=lats, lons=lons), gri...  11.6 us
    ppermute x3, starting transfers between devices, cell_step(): lax.ppermute(p, ('lon', 'lat'), pairs(k, 1 < k < lons - 1))  9.37 us
    unnamed x30, local copies, waits for them, and re-layouts  8.67 us
    pallas_call x1, Pallas kernels, update_call(): pl.pallas_call(update_kernel, grid=(rows // block,), in_specs=[pl.BlockSp...  8.25 us
    pallas_call x1, Pallas kernels, node_call(): pl.pallas_call(node_kernel, in_specs=[local] * 9, out_specs=local, out_sh...  1.34 us
  transfers between devices with their start and end apart: 3, of which 0 were waited for; matrix products, arithmetic and copies ran while one was open for 0% of the time, Pallas kernels for 33%

commit v1 on v0

--- a/solution.py
+++ b/solution.py
@@ -12,6 +12,10 @@
 FEATS = 16
 TILE = 32
 SUB = 256
+PREP = 256
+PACK_VMEM = 40 * 2 ** 20
+PACK_FLOPS = 2 * 10 ** 9
+PACK_BYTES = 10 ** 6
 EDGE_VMEM = 20 * 2 ** 20
 NODE_VMEM = 6 * 2 ** 20
 GRID_VMEM = 24 * 2 ** 20
@@ -82,9 +86,26 @@
         table[:, 128 * p:128 * (p + 1)] = pieces[p] + pltpu.roll(pieces[p + nodes // 2], 64, 1)
 
 
-def embed_kernel(x_ref, wg_ref, w0_ref, bg_ref, send_ref, mask_ref, edge_ref, mesh_ref,
+def pack_kernel(send_ref, mask_ref, edge_ref, mesh_ref, out_ref, lanes, table, *, grid_cols):
+    pack_slots(send_ref, mask_ref, edge_ref, mesh_ref, lanes, table, lax.axis_index('lon'), grid_cols)
+    out_ref[...] = table[...].astype(BF16)
+
+
+def pack_call(senders, edge_mask, edge_t, mesh_t, grid_cols):
+    width = senders.shape[0] // 2 * 128
+    return pl.pallas_call(
+        functools.partial(pack_kernel, grid_cols=grid_cols),
+        out_shape=jax.ShapeDtypeStruct((FEATS, width), BF16),
+        scratch_shapes=[pltpu.VMEM((FEATS, 128), F32), pltpu.VMEM((FEATS, width), F32)],
+        compiler_params=pltpu.CompilerParams(vmem_limit_bytes=PACK_VMEM),
+        cost_estimate=pl.CostEstimate(flops=PACK_FLOPS, transcendentals=0, bytes_accessed=PACK_BYTES),
+        name='pack',
+    )(senders, edge_mask, edge_t, mesh_t)
+
+
+def embed_kernel(x_ref, wg_ref, w0_ref, bg_ref, feat_ref,
                  vg_ref, tab_ref, band_ref,
-                 scr, half, lanes, table, feat_ref, up_buf, down_buf, from_south, from_north, feat_in, up_sems, down_sems, feat_send, feat_recv, *, lats, lons):
+                 scr, half, up_buf, down_buf, from_south, from_north, feat_in, up_sems, down_sems, feat_send, feat_recv, *, lats, lons):
     batch, grid_rows, cols, chans = x_ref.shape
     latent = vg_ref.shape[-1]
     step = pl.program_id(0)
@@ -119,9 +140,6 @@
         def _():
             pl.semaphore_signal(barrier, 1, device_id={'lat': lat + 1}, device_id_type=mesh_id)
 
-        pack_slots(send_ref, mask_ref, edge_ref, mesh_ref, lanes, table, lon, cols * lons)
-        feat_ref[...] = table[...].astype(BF16)
-
     @pl.when(step == 1)
     def _():
         barrier = pltpu.get_barrier_semaphore()
@@ -186,12 +204,10 @@
             tab_ref[grid_rows + REACH:grid_rows + 2 * REACH] = from_south[...]
 
 
-def embed_call(grid_in, w_grid, w_out, bias_gain, senders, edge_mask, edge_t, mesh_t, lats, lons, block):
+def embed_call(grid_in, w_grid, w_out, bias_gain, feats, lats, lons, block):
     batch, rows, cols, chans = grid_in.shape
     latent = w_out.shape[-1]
     steps = rows // block
-    nodes = senders.shape[0]
-    feats = jax.ShapeDtypeStruct((FEATS, nodes // 2 * 128), BF16)
     whole = lambda *shape: pl.BlockSpec(shape, lambda r: (0,) * len(shape))
     pick = lambda k, *shape: pl.BlockSpec((1,) + shape, lambda r: (k,) + (0,) * len(shape))
     strip = (REACH, cols, batch, latent)
@@ -201,8 +217,7 @@
         grid=(steps,),
         in_specs=[
             local,
-            whole(chans, latent), pick(0, latent, latent), pick(0, 4, latent), whole(*senders.shape),
-            whole(*edge_mask.shape), whole(*edge_t.shape), whole(*mesh_t.shape)],
+            whole(chans, latent), pick(0, latent, latent), pick(0, 4, latent), local],
         out_specs=[local, local, local],
         out_shape=[
             jax.ShapeDtypeStruct((batch, rows, cols, latent), BF16),
@@ -210,8 +225,7 @@
             jax.ShapeDtypeStruct((lons,) + feats.shape, BF16)],
         scratch_shapes=[
             pltpu.VMEM((block, latent // 128, batch * (cols + 8), 128), F32),
-            pltpu.VMEM((chans, latent), BF16), pltpu.VMEM((FEATS, 128), F32), pltpu.VMEM(feats.shape, F32),
-            pltpu.VMEM(feats.shape, BF16),
+            pltpu.VMEM((chans, latent), BF16),
             pltpu.VMEM(strip, BF16), pltpu.VMEM(strip, BF16), pltpu.VMEM(strip, BF16), pltpu.VMEM(strip, BF16),
             pltpu.VMEM((lons,) + feats.shape, BF16),
             pltpu.SemaphoreType.DMA((2,)), pltpu.SemaphoreType.DMA((2,)),
@@ -221,7 +235,7 @@
             flops=4 * rows * batch * cols * latent * latent, transcendentals=0,
             bytes_accessed=6 * rows * batch * cols * latent),
         name='embed',
-    )(grid_in, w_grid, w_out, bias_gain, senders, edge_mask, edge_t, mesh_t)
+    )(grid_in, w_grid, w_out, bias_gain, feats)
 
 
 def halve(dst, src):
@@ -275,17 +289,52 @@
     )(vg, w_gupd, w_out, bias_gain, dep)
 
 
-def edge_kernel(v_ref, we_ref, wm_ref, wmsg_ref, wo_ref, wn_ref, bg_ref,
-                tab_ref, *rest, lats, lons, near):
-    lp, ec, vmf, idx_v, idx_s, part, half, hid_a, hid_b, xbuf, isem = rest[-11:]
-    outs = rest[:-11]
+def message_loop(start, stop, tab_ref, w_in, w3, bg3, lp, ec, idx, part, bufs, hids):
+    rows, cols, batch, latent = tab_ref.shape
+    table = tab_ref.reshape(rows * cols, batch, latent)
+    per = TILE // 2
+    b2 = bg3[1:2]
+    gain = bg3[2:3]
+
+    def first(base, k):
+        for s in range(per):
+            bufs[k][pl.ds(s * batch, batch), :] = table[idx[0, base + s]]
+        here = pl.ds(pl.multiple_of(base, per), per)
+        acc = mm(bufs[k][...], w_in[...]).reshape(per, batch, latent)
+        hids[k][...] = gate(acc + lp[here, :].reshape(per, 1, latent)).reshape(per * batch, latent)
+
+    def second(base, k):
+        here = pl.ds(pl.multiple_of(base, per), per)
+        y = mm(hids[k][...], w3[...]) + b2
+        z = (norm(y) * gain).reshape(per, batch, latent) + ec[here, :].reshape(per, 1, latent)
+        z = z.astype(BF16).astype(F32)
+        for s in range(per):
+            n = idx[1, base + s]
+            part[n] += z[s]
+
+    @pl.when(stop > start)
+    def _():
+        first(start * TILE, 0)
+
+    def step(t, carry):
+        base = t * TILE
+        first(base + per, 1)
+        second(base, 0)
+        first(jnp.minimum(t + 1, stop - 1) * TILE, 0)
+        second(base + per, 1)
+        return carry
+
+    lax.fori_loop(start, stop, step, 0)
+
+
+def far_kernel(v_ref, we_ref, wm_ref, wmsg_ref, wo_ref, bg_ref, tab_ref,
+               p1_ref, p2_ref, p3_ref, lp, ec, idx_v, own_vm_ref,
+               vmf, idx_s, part, half, hid_a, hid_b, buf_a, buf_b, isem, *, lons, nodes):
     latent = wo_ref.shape[-1]
     slots = lons * v_ref.shape[-1]
-    grid_rows, cols, batch = tab_ref.shape[:3]
+    grid_rows, cols = tab_ref.shape[:2]
     positions = grid_rows * cols
     cell_rows = grid_rows - 2 * REACH
-    table = tab_ref.reshape(positions, batch, latent)
-    nodes = outs[0].shape[0]
     band = lons * nodes
     lat = lax.axis_index('lat')
     lon = lax.axis_index('lon')
@@ -303,142 +352,143 @@
     bg2 = bg_ref[2]
     bg3 = bg_ref[3]
     vm = mlp_tail(mm(mesh_feat, wm) + bg1[0:1], wo_ref[1], bg1).astype(BF16)
-    if near:
-        vmf[...] = vm.astype(F32)
-        own_vm = vmf[pl.ds(pl.multiple_of(lon * nodes, 8), nodes), :]
-        outs[1][...] = own_vm
-        outs[2][...] = mm(own_vm.astype(BF16), wn_ref[0:latent, :]) + bg_ref[4][0:1]
+    vmf[...] = vm.astype(F32)
+    own_vm_ref[...] = vmf[pl.ds(pl.multiple_of(lon * nodes, 8), nodes), :]
 
     col = vt[5:6] - (lon * cols).astype(F32)
     cell = vt[7:8] - (lon * nodes).astype(F32)
     inner = (cell > -0.5) & (cell < nodes - 0.5)
-    wanted = inner if near else jnp.logical_not(inner)
-    flag = jnp.where((vt[6:7] > 0.5) & (col > -0.5) & (col < cols - 0.5) & wanted, 1.0, 0.0)
+    live = (vt[6:7] > 0.5) & (col > -0.5) & (col < cols - 0.5)
     chunks = slots // 128
-    pad = -chunks % 16
-    rows = [flag[:, 128 * c:128 * (c + 1)] for c in range(chunks)] + [jnp.zeros((pad, 128), F32)] * (pad > 0)
-    flags = jnp.concatenate(rows, axis=0)
     up = lax.broadcasted_iota(jnp.int32, (128, 128), 0) <= lax.broadcasted_iota(jnp.int32, (128, 128), 1)
-    incl = mm(flags.astype(BF16), jnp.where(up, 1.0, 0.0).astype(BF16))
-    n_rows = chunks + pad
-    low = lax.broadcasted_iota(jnp.int32, (n_rows, n_rows), 1) < lax.broadcasted_iota(jnp.int32, (n_rows, n_rows), 0)
-    row_sum = jnp.broadcast_to(incl[:, 127:128], (n_rows, 128)).astype(BF16)
-    before = mm(jnp.where(low, 1.0, 0.0).astype(BF16), row_sum)
-    rank = jnp.where(flags > 0.5, incl + before - 1.0, -1.0)
-    total = jnp.sum(flag).astype(jnp.int32)
-
-    def prep(t, carry):
-        slot = (lax.broadcasted_iota(jnp.int32, (128, 128), 0) + t * 128).astype(F32)
-        sel = jnp.concatenate(
+    low = lax.broadcasted_iota(jnp.int32, (chunks, chunks), 1) < lax.broadcasted_iota(jnp.int32, (chunks, chunks), 0)
+    up = jnp.where(up, 1.0, 0.0).astype(BF16)
+    low = jnp.where(low, 1.0, 0.0).astype(BF16)
+
+    def ranks(flag):
+        flag = jnp.where(flag, 1.0, 0.0)
+        flags = jnp.concatenate([flag[:, 128 * c:128 * (c + 1)] for c in range(chunks)], axis=0)
+        incl = mm(flags.astype(BF16), up)
+        before = mm(low, jnp.broadcast_to(incl[:, 127:128], (chunks, 128)).astype(BF16))
+        return flags, incl + before - 1.0, jnp.sum(flag).astype(jnp.int32)
+
+    far, far_rank, n_far = ranks(live & jnp.logical_not(inner))
+    near, near_rank, n_near = ranks(live & inner)
+    far_tiles = lax.div(n_far + TILE - 1, TILE)
+    skip = far_tiles * TILE
+    end = skip + n_near
+    rank = jnp.where(far > 0.5, far_rank, jnp.where(near > 0.5, near_rank + skip.astype(F32), -1.0))
+    preps = lax.div(end + PREP - 1, PREP)
+
+    def select(t):
+        slot = (lax.broadcasted_iota(jnp.int32, (PREP, 128), 0) + t * PREP).astype(F32)
+        return jnp.concatenate(
             [jnp.where(rank[c:c + 1] == slot, 1.0, 0.0).astype(BF16) for c in range(chunks)], axis=1)
-        feat = mm_nt(sel, vtb).astype(BF16)
-        feat_t = mm_nt(vtb, sel)
-        here = pl.ds(pl.multiple_of(t * 128, 128), 128)
-        live = lax.broadcasted_iota(jnp.int32, (1, 128), 1) + t * 128 < total
+
+    def index(t, carry):
+        feat_t = mm_nt(vtb, select(t))
+        here = pl.ds(pl.multiple_of(t * PREP, PREP), PREP)
+        slot = lax.broadcasted_iota(jnp.int32, (1, PREP), 1) + t * PREP
+        used = (slot < n_far) | ((slot >= skip) & (slot < end))
         win_r = feat_t[4:5] - (lat * cell_rows - REACH).astype(F32)
         win_c = feat_t[5:6] - (lon * cols).astype(F32)
-        pos = jnp.where(live, (win_r * cols + win_c).astype(jnp.int32), REACH * cols)
-        node = feat_t[7:8].astype(jnp.int32)
-        rel = lax.rem(node + (lons - lon) * nodes, band)
+        pos = jnp.where(used, (win_r * cols + win_c).astype(jnp.int32), REACH * cols)
+        rel = lax.rem(feat_t[7:8].astype(jnp.int32) + (lons - lon) * nodes, band)
         idx_v[0:1, here] = jnp.clip(pos, 0, positions - 1)
-        idx_v[1:2, here] = jnp.where(live, rel, band)
+        idx_v[1:2, here] = jnp.where(used, rel, band)
+        idx_v[2:3, here] = jnp.full((1, PREP), far_tiles, jnp.int32)
+        idx_v[3:4, here] = jnp.full((1, PREP), lax.div(end + TILE - 1, TILE), jnp.int32)
+        return carry
+
+    idx_v[2:3, 0:128] = jnp.zeros((1, 128), jnp.int32)
+    idx_v[3:4, 0:128] = jnp.zeros((1, 128), jnp.int32)
+    lax.fori_loop(0, preps, index, 0)
+    move = pltpu.make_async_copy(idx_v, idx_s, isem)
+    move.start()
+    part[...] = jnp.zeros_like(part)
+    half[...] = wmsg_ref[latent:2 * latent, :] * jnp.asarray(0.5, BF16)
+
+    def prep(t, carry):
+        feat = mm_nt(select(t), vtb).astype(BF16)
+        here = pl.ds(pl.multiple_of(t * PREP, PREP), PREP)
         edge = mlp_tail(mm(feat, we) + bg2[0:1], wo_ref[2], bg2).astype(BF16)
-        node_col = feat[:, 7:8].astype(F32)
-        hot = lax.broadcasted_iota(jnp.int32, (128, band), 1).astype(F32) == node_col
+        hot = lax.broadcasted_iota(jnp.int32, (PREP, band), 1).astype(F32) == feat[:, 7:8].astype(F32)
         vm_e = mm(jnp.where(hot, 1.0, 0.0).astype(BF16), vm).astype(BF16)
         lp[here, :] = (mm(edge, wmsg_ref[0:latent, :]) + mm(vm_e, wmsg_ref[2 * latent:, :]) + bg3[0:1]) * 0.5
         ec[here, :] = edge.astype(F32) + bg3[3:4]
         return carry
 
-    lax.fori_loop(0, lax.div(total + 127, 128), prep, 0)
-    move = pltpu.make_async_copy(idx_v, idx_s, isem)
-    move.start()
+    lax.fori_loop(0, preps, prep, 0)
+    move.wait()
+    message_loop(0, far_tiles, tab_ref, half, wo_ref.at[3], bg3, lp, ec, idx_s, part, (buf_a, buf_b), (hid_a, hid_b))
+    for k, ref in enumerate((p1_ref, p2_ref, p3_ref)):
+        ref[...] = part[(k + 1) * nodes:(k + 2) * nodes]
+
+
+def near_kernel(idx, lp, ec, wmsg_ref, wo_ref, bg_ref, tab_ref, own_ref, part, half, hid_a, hid_b, buf_a, buf_b):
+    latent = wo_ref.shape[-1]
+    nodes = own_ref.shape[0]
     part[...] = jnp.zeros_like(part)
     half[...] = wmsg_ref[latent:2 * latent, :] * jnp.asarray(0.5, BF16)
-    move.wait()
-
-    per = TILE // 2
-    bufs = (xbuf.at[0], xbuf.at[1])
-    hids = (hid_a, hid_b)
-
-    def first(base, k):
-        for s in range(per):
-            bufs[k][pl.ds(s * batch, batch), :] = table[idx_s[0, base + s]]
-        acc = mm(bufs[k][...], half[...]).reshape(per, batch, latent)
-        here = pl.ds(pl.multiple_of(base, per), per)
-        hids[k][...] = gate(acc + lp[here, :].reshape(per, 1, latent)).reshape(per * batch, latent)
-
-    def second(base, k):
-        y = mm(hids[k][...], wo_ref[3]) + bg3[1:2]
-        here = pl.ds(pl.multiple_of(base, per), per)
-        z = (norm(y) * bg3[2:3]).reshape(per, batch, latent) + ec[here, :].reshape(per, 1, latent)
-        z = z.astype(BF16).astype(F32)
-        for s in range(per):
-            n = idx_s[1, base + s]
-            part[n] += z[s]
-
-    tiles = lax.div(total + TILE - 1, TILE)
-
-    @pl.when(tiles > 0)
-    def _():
-        first(0, 0)
-
-    def edges(t, carry):
-        base = t * TILE
-        first(base + per, 1)
-        second(base, 0)
-        first(jnp.minimum(t + 1, tiles - 1) * TILE, 0)
-        second(base + per, 1)
-        return carry
-
-    lax.fori_loop(0, tiles, edges, 0)
-    if near:
-        outs[0][...] = part[0:nodes]
-    else:
-        for k in range(1, lons):
-            outs[k - 1][...] = part[k * nodes:(k + 1) * nodes]
-
-
-def edge_call(v, w_edge, w_mesh, w_msg, w_out, w_node, bias_gain, table, lats, lons, nodes, per_node, near):
+    message_loop(idx[2, 0], idx[3, 0], tab_ref, half, wo_ref.at[3], bg_ref[3], lp, ec, idx, part,
+                 (buf_a, buf_b), (hid_a, hid_b))
+    own_ref[...] = part[0:nodes]
+
+
+def loop_scratch(batch, latent):
+    half_tile = pltpu.VMEM((TILE // 2 * batch, latent), BF16)
+    return [pltpu.VMEM((latent, latent), BF16)] + [half_tile] * 4
+
+
+def edge_call(v, w_edge, w_mesh, w_msg, w_out, bias_gain, table, lats, lons, nodes, per_node):
     latent = w_out.shape[-1]
-    slots = lons * v.shape[-1]
     batch = table.shape[2]
-    whole = lambda a: pl.BlockSpec(a.shape, lambda r: (0,) * a.ndim)
-    pick = lambda k, *shape: pl.BlockSpec((1,) + shape, lambda r: (k,) + (0,) * len(shape))
-    limit = lons * nodes * per_node
-    block = jax.ShapeDtypeStruct((nodes, batch, latent), F32)
-    row = jax.ShapeDtypeStruct((nodes, latent), F32)
-    outs = [block] + [row] * 2 if near else [block] * (lons - 1)
+    limit = lons * nodes * per_node + PREP
     local = pl.BlockSpec(memory_space=pltpu.VMEM)
-    return pl.pallas_call(
-        functools.partial(edge_kernel, lats=lats, lons=lons, near=near),
-        in_specs=[local] * 8,
+    outs = [jax.ShapeDtypeStruct((nodes, batch, latent), F32)] * (lons - 1)
+    outs += [jax.ShapeDtypeStruct((limit, latent), F32)] * 2
+    outs += [jax.ShapeDtypeStruct((4, limit), jnp.int32), jax.ShapeDtypeStruct((nodes, latent), F32)]
+    res = pl.pallas_call(
+        functools.partial(far_kernel, lons=lons, nodes=nodes),
+        in_specs=[local] * 7,
         out_specs=[local] * len(outs),
         out_shape=outs,
         scratch_shapes=[
-            pltpu.VMEM((limit, latent), F32),
-            pltpu.VMEM((limit, latent), F32),
             pltpu.VMEM((lons * nodes, latent), F32),
-            pltpu.VMEM((8, limit), jnp.int32),
-            pltpu.SMEM((8, limit), jnp.int32),
-            pltpu.VMEM((lons * nodes + 1, batch, latent), F32),
-            pltpu.VMEM((latent, latent), BF16),
-            pltpu.VMEM((TILE // 2 * batch, latent), BF16),
-            pltpu.VMEM((TILE // 2 * batch, latent), BF16),
-            pltpu.VMEM((2, TILE // 2 * batch, latent), BF16),
-            pltpu.SemaphoreType.DMA],
+            pltpu.SMEM((4, limit), jnp.int32),
+            pltpu.VMEM((lons * nodes + 1, batch, latent), F32)] + loop_scratch(batch, latent) + [pltpu.SemaphoreType.DMA],
+        compiler_params=pltpu.CompilerParams(vmem_limit_bytes=EDGE_VMEM),
         cost_estimate=pl.CostEstimate(
-            flops=4 * slots // 4 * batch * latent * latent, transcendentals=0, bytes_accessed=2 * slots * batch * latent),
+            flops=4 * limit // 8 * batch * latent * latent, transcendentals=0, bytes_accessed=limit * batch * latent),
+        name='edges_far',
+    )(v, w_edge, w_mesh, w_msg, w_out, bias_gain, table)
+    return res[:lons - 1], (res[-2], res[-4], res[-3], res[-1])
+
+
+def near_call(lists, w_msg, w_out, bias_gain, table, nodes, band):
+    idx, lp, ec, _ = lists
+    latent = w_out.shape[-1]
+    batch = table.shape[2]
+    local = pl.BlockSpec(memory_space=pltpu.VMEM)
+    return pl.pallas_call(
+        near_kernel,
+        in_specs=[pl.BlockSpec(memory_space=pltpu.SMEM)] + [local] * 6,
+        out_specs=[local],
+        out_shape=[jax.ShapeDtypeStruct((nodes, batch, latent), F32)],
+        scratch_shapes=[pltpu.VMEM((band + 1, batch, latent), F32)] + loop_scratch(batch, latent),
         compiler_params=pltpu.CompilerParams(vmem_limit_bytes=EDGE_VMEM),
-        name='edges_near' if near else 'edges_far',
-    )(v, w_edge, w_mesh, w_msg, w_out, w_node, bias_gain, table)
-
-
-def node_kernel(own_ref, r1_ref, r2_ref, r3_ref, vm_ref, nb_ref, wn_ref, w4_ref, bg_ref, out_ref, scr):
+        cost_estimate=pl.CostEstimate(
+            flops=lp.shape[0] * batch * latent * latent, transcendentals=0, bytes_accessed=lp.shape[0] * batch * latent),
+        name='edges_near',
+    )(idx, lp, ec, w_msg, w_out, bias_gain, table)
+
+
+def node_kernel(own_ref, r1_ref, r2_ref, r3_ref, vm_ref, wn_ref, w4_ref, bg_ref, out_ref, scr):
     nodes, batch, latent = own_ref.shape
     agg = (own_ref[...] + r1_ref[...] + r2_ref[...] + r3_ref[...]).astype(BF16).reshape(nodes * batch, latent)
-    acc = mm(agg, wn_ref[latent:, :]).reshape(nodes, batch, latent) + nb_ref[...].reshape(nodes, 1, latent)
     bg = bg_ref[4]
+    base = mm(vm_ref[...].astype(BF16), wn_ref[0:latent, :]) + bg[0:1]
+    acc = mm(agg, wn_ref[latent:, :]).reshape(nodes, batch, latent) + base.reshape(nodes, 1, latent)
     upd = mlp_tail(acc.reshape(nodes * batch, latent), w4_ref[4], bg)
     out = (upd.reshape(nodes, batch, latent) + vm_ref[...].reshape(nodes, 1, latent)).reshape(nodes * batch, latent)
 
@@ -448,19 +498,19 @@
     swap_rows(out, scr, batch, put)
 
 
-def node_call(blocks, vm, nb, w_node, w_out, bias_gain):
+def node_call(blocks, vm, w_node, w_out, bias_gain):
     nodes, batch, latent = blocks[0].shape
     local = pl.BlockSpec(memory_space=pltpu.VMEM)
     out = jax.ShapeDtypeStruct((batch, nodes, latent), BF16)
     return pl.pallas_call(
         node_kernel,
-        in_specs=[local] * 9,
+        in_specs=[local] * 8,
         out_specs=local,
         out_shape=out,
         compiler_params=pltpu.CompilerParams(vmem_limit_bytes=NODE_VMEM),
         scratch_shapes=[pltpu.VMEM((latent // 128, nodes * (batch + 8), 128), F32)],
         name='nodes',
-    )(*blocks, vm, nb, w_node, w_out, bias_gain)
+    )(*blocks, vm, w_node, w_out, bias_gain)
 
 
 def solution(mesh):
@@ -473,19 +523,17 @@
         batch, rows, cols, _ = grid_in.shape
         nodes = senders.shape[0]
         latent = w_out.shape[-1]
-        vg, table, band = embed_call(
-            grid_in, w_grid, w_out, bias_gain, senders, edge_mask, jnp.swapaxes(edge_in, 1, 2), mesh_in.T, lats, lons, 4)
-        edges = functools.partial(
-            edge_call, band, w_edge, w_mesh, w_msg, w_out, w_node, bias_gain, table, lats, lons, *senders.shape)
-        p1, p2, p3 = edges(False)
-        own, vm, nb = edges(True)
+        feats = pack_call(senders, edge_mask, jnp.swapaxes(edge_in, 1, 2), mesh_in.T, cols * lons)
+        vg, table, band = embed_call(grid_in, w_grid, w_out, bias_gain, feats, lats, lons, 4)
+        blocks, lists = edge_call(band, w_edge, w_mesh, w_msg, w_out, bias_gain, table, lats, lons, *senders.shape)
+        own, = near_call(lists, w_msg, w_out, bias_gain, table, senders.shape[0], senders.shape[0] * lons)
         pairs = lambda k, polar: [
             (j * lats + i, (j + k) % lons * lats + i) for i in range(lats) for j in range(lons)
             if not polar or i in (0, lats - 1)]
-        got = [lax.ppermute(p, ('lon', 'lat'), pairs(k, 1 < k < lons - 1)) for k, p in ((2, p2), (1, p1), (3, p3))]
-        flat = update_call(vg.reshape(batch * rows * cols, latent), w_gupd, w_out, bias_gain, nb, 1024)
+        got = [lax.ppermute(p, ('lon', 'lat'), pairs(k, 1 < k < lons - 1)) for k, p in ((2, blocks[1]), (1, blocks[0]), (3, blocks[2]))]
+        flat = update_call(vg.reshape(batch * rows * cols, latent), w_gupd, w_out, bias_gain, own, 1024)
         grid_out = flat.reshape(batch, rows, cols, latent)
-        mesh_out = node_call([own] + got, vm, nb, w_node, w_out, bias_gain)
+        mesh_out = node_call([own] + got, lists[3], w_node, w_out, bias_gain)
         return mesh_out, grid_out
 
     grid_spec = P('dp', 'lat', 'lon', None)

time: 58.8 us -> 50.2 us (0.85); the launches traced: 59.5 us -> 49.9 us
  local copies, waits for them, and re-layouts: 8.67 us -> 4.58 us
  Pallas kernels: 40.6 us -> 37.5 us
  starting transfers between devices: 9.37 us -> 7.02 us
    unnamed x30 -> x26, local copies, waits for them, and re-layouts: 8.67 us -> 4.58 us
    pallas_call x3 -> x4, Pallas kernels: 20.8 us -> 18.1 us  [the longest x1 10.7 us: edge_call(): pl.pallas_call(functools.partial(far_kernel, lons=lons, nodes=nodes), in_...]
    ppermute x3, starting transfers between devices: 9.37 us -> 7.02 us  [cell_step(): lax.ppermute(p, ('lon', 'lat'), pairs(k, 1 < k < lons - 1))]
  transfers between devices with their start and end apart: 3 -> 3, of which waited for: 0 -> 0; matrix products, arithmetic and copies ran while one was open for 0% -> 0% of each run, Pallas kernels for 33% -> 28%
where the time goes in v1:
time: 50.2 us; the launch traced here: 49.9 us
  Pallas kernels  37.5 us (75%)
  starting transfers between devices  7.02 us (14%)
  local copies, waits for them, and re-layouts  4.58 us (9%)
  between operations  0.77 us (2%)
    pallas_call x1, Pallas kernels, embed_call(): pl.pallas_call(functools.partial(embed_kernel, lats=lats, lons=lons), gri...  11.5 us
    pallas_call x1, Pallas kernels, edge_call(): pl.pallas_call(functools.partial(far_kernel, lons=lons, nodes=nodes), in_...  10.7 us
    pallas_call x1, Pallas kernels, update_call(): pl.pallas_call(update_kernel, grid=(rows // block,), in_specs=[pl.BlockSp...  7.94 us
    ppermute x3, starting transfers between devices, cell_step(): lax.ppermute(p, ('lon', 'lat'), pairs(k, 1 < k < lons - 1))  7.02 us
    pallas_call x1, Pallas kernels, near_call(): pl.pallas_call(near_kernel, in_specs=[pl.BlockSpec(memory_space=pltpu.SME...  5.79 us
    unnamed x26, local copies, waits for them, and re-layouts  4.58 us
    pallas_call x1, Pallas kernels, node_call(): pl.pallas_call(node_kernel, in_specs=[local] * 8, out_specs=local, out_sh...  1.39 us
  transfers between devices with their start and end apart: 3, of which 0 were waited for; matrix products, arithmetic and copies ran while one was open for 0% of the time, Pallas kernels for 28%

profile of v1, /device:TPU:0, one launch (start us, length us, event | category | flops | bytes accessed | tf_op | source)
XLA Modules:
  0.0 49.9 jit_solution(13028187073935880495)
XLA Ops:
  0.6 0.0 copy-start.2
  0.6 0.0 copy-start
  0.7 0.0 copy-start.3
  0.7 0.0 copy-start.7
  0.7 0.8 %copy-done.7 = bf16[8,48,4]{1,2,0:T(4,128)(2,1)S(1)} copy-done((bf16[8,48,4]{1,2,0:T(4,128)(2,1)S(1)}, bf16[8,48,4]{1,2,0:T(4,128)(2,1)}, u32[]{:S(2)}) %copy-start.7) | copy-done | bytes 3096
  1.5 0.0 copy-start.8
  1.5 1.1 %copy-done.8 = s32[8,48]{1,0:T(8,128)S(1)} copy-done((s32[8,48]{1,0:T(8,128)S(1)}, s32[8,48]{1,0:T(8,128)}, u32[]{:S(2)}) %copy-start.8) | copy-done | bytes 1560
  2.6 0.0 copy-start.9
  2.6 0.9 %copy-done.9 = s32[8,48]{1,0:T(8,128)S(1)} copy-done((s32[8,48]{1,0:T(8,128)S(1)}, s32[8,48]{1,0:T(8,128)}, u32[]{:S(2)}) %copy-start.9) | copy-done | bytes 1560
  3.5 0.0 copy-start.12
  3.5 0.7 %copy-done.12 = bf16[8,3]{0,1:T(4,128)(2,1)S(1)} copy-done((bf16[8,3]{0,1:T(4,128)(2,1)S(1)}, bf16[8,3]{0,1:T(4,128)(2,1)}, u32[]{:S(2)}) %copy-start.12) | copy-done | bytes 72
  4.2 0.2 pack.1.feat_ref
  4.4 0.0 copy-done.2
  4.4 0.0 copy-done
  4.4 0.0 copy-done.3
  4.4 0.0 copy-start.6
  4.4 1.0 %copy-done.6 = bf16[474,512]{1,0:T(8,128)(2,1)S(1)} copy-done((bf16[474,512]{1,0:T(8,128)(2,1)S(1)}, bf16[474,512]{1,0:T(8,128)(2,1)}, u32[]{:S(2)}) %copy-start.6) | copy-done | bytes 485400
  5.4 0.0 copy-start.4
  5.4 0.0 copy-start.10
  5.4 0.0 copy-start.11
  5.4 11.5 %embed.1 = (bf16[16,16,16,512]{3,2,1,0:T(8,128)(2,1)S(1)}, bf16[22,16,16,512]{3,2,1,0:T(8,128)(2,1)S(1)}, bf16[4,16,512]{2,1,0:T(8,128)(2,1)S(1)}) custom-call(bf16[16,16,16,474]{3,2,1,0:T(8,128)(2,1)S(1)} %copy-done.3, bf16[474,512]{1,0:T(8,128)(2,1)S(1)} %copy-done.6, bf16[6,512,512]{2,1,0:T(8,128)(2,1)S(1)} %copy-done, f32[6,4,512]{2,1,0:T(4,128)S(1)} %copy-done.2, ...), custom_call_target="tpu_custom_call" | custom-call | flops 4294967296 | bytes 12582912 | tf_op jit(solution)/shard_map/embed/pallas_call | solution.py:215
  17.0 0.0 copy-done.4
  17.0 0.0 copy-done.10
  17.0 0.0 copy-done.11
  17.0 10.7 %edges_far.1 = (f32[8,16,512]{2,1,0:T(8,128)S(1)}, f32[8,16,512]{2,1,0:T(8,128)S(1)}, f32[8,16,512]{2,1,0:T(8,128)S(1)}, f32[1792,512]{1,0:T(8,128)S(1)}, f32[17...) custom-call(bf16[4,16,512]{2,1,0:T(8,128)(2,1)S(1)} %get-tuple-element.12.v_ref, ...), custom_call_target="tpu_custom_call" | custom-call | flops 3758096384 | bytes 14680064 | tf_op jit(solution)/shard_map/edges_far/pallas_call | solution.py:451
  27.7 3.1 %collective-permute-start = (f32[8,16,512]{2,1,0:T(8,128)S(1)}, f32[8,16,512]{2,1,0:T(8,128)S(1)}, u32[]{:S(2)}, u32[]{:S(2)}) collective-permute-start(f32[8,16,512]{2,1,0:T(8,128)S(1)} %get-tuple-element.17), channel_id=1, source_target_pairs={{0,8},{4,12},{8,0},{12,4},{3,11},{7,15},{11,3},{15,7},{16,24},{20,... | collective-permute-start | bytes 786440 | tf_op jit(solution)/shard_map/ppermute | solution.py:533
  30.8 1.6 %collective-permute-start.1 = (f32[8,16,512]{2,1,0:T(8,128)S(1)}, f32[8,16,512]{2,1,0:T(8,128)S(1)}, u32[]{:S(2)}, u32[]{:S(2)}) collective-permute-start(f32[8,16,512]{2,1,0:T(8,128)S(1)} %get-tuple-element.18), channel_id=1, source_target_pairs={{0,4},{4,8},{8,12},{12,0},{1,5},{5,9},{9,13},{13,1},{2,6},{6,10},{... | collective-permute-start | bytes 786440 | tf_op jit(solution)/shard_map/ppermute | solution.py:533
  32.5 2.2 %collective-permute-start.2 = (f32[8,16,512]{2,1,0:T(8,128)S(1)}, f32[8,16,512]{2,1,0:T(8,128)S(1)}, u32[]{:S(2)}, u32[]{:S(2)}) collective-permute-start(f32[8,16,512]{2,1,0:T(8,128)S(1)} %get-tuple-element.19), channel_id=1, source_target_pairs={{0,12},{4,0},{8,4},{12,8},{1,13},{5,1},{9,5},{13,9},{2,14},{6,2},{... | collective-permute-start | bytes 786440 | tf_op jit(solution)/shard_map/ppermute | solution.py:533
  34.7 0.0 copy-start.5
  34.7 5.8 %edges_near.1.own_ref.dep_ref = f32[8,16,512]{2,1,0:T(8,128)S(1)} custom-call(s32[4,1792]{1,0:T(4,128)S(1)} %get-tuple-element.14.idx, f32[1792,512]{1,0:T(8,128)S(1)} %get-tuple-element.15.lp, f32[1792,512]{1,0:T(8,128)S(1)} %get-tuple-element.16.ec, bf16[1536,512]{1,0:T(8,128)(2,1)S(1)} %copy-done.4, bf16[6,512,512]{2,1,0:T(8,128)(2,1)S(1)} %copy-done, ...), custom_call_target="tpu_custom_call" | custom-call | flops 7516192768 | bytes 14680064 | tf_op jit(solution)/shard_map/edges_near/pallas_call | solution.py:473
  40.5 0.0 copy-done.5
  40.5 0.0 copy-start.1
  40.5 7.9 %update.1 = bf16[4096,512]{1,0:T(8,128)(2,1)} custom-call(bf16[4096,512]{1,0:T(8,128)(2,1)S(1)} %bitcast.6, bf16[512,512]{1,0:T(8,128)(2,1)S(1)} %copy-done.5, bf16[6,512,512]{2,1,0:T(8,128)(2,1)S(1)} %copy-done, f32[6,4,512]{2,1,0:T(4,128)S(1)} %copy-done.2, f32[8,16,512]{2,1,0:T(8,128)S(1)} %edges_near.1.own_ref.dep_ref), custom_call_target="tpu_custom_call" | custom-call | flops 4294967296 | bytes 8388608 | tf_op jit(solution)/shard_map/update/pallas_call | solution.py:278
  48.5 0.0 collective-permute-done.r1_ref
  48.5 0.0 collective-permute-done.1.r2_ref
  48.5 0.0 collective-permute-done.2.r3_ref
  48.5 0.0 copy-done.1
  48.5 1.4 %nodes.1 = bf16[16,8,512]{2,1,0:T(8,128)(2,1)} custom-call(f32[8,16,512]{2,1,0:T(8,128)S(1)} %edges_near.1.own_ref.dep_ref, f32[8,16,512]{2,1,0:T(8,128)S(1)} %collective-permute-done.r1_ref, f32[8,16,512]{2,1,0:T(8,128)S(1)} %collective-permute-done.1.r2_ref, f32[8,16,512]{2,1,0:T(8,128)S(1)} %collective-permute-done.2.r3_ref, ...), custom_call_target="tpu_custom_call" | custom-call | tf_op jit(solution)/shard_map/nodes/pallas_call | solution.py:505
Async XLA Ops:
  0.6 3.8 %copy-start.2 = (f32[6,4,512]{2,1,0:T(4,128)S(1)}, f32[6,4,512]{2,1,0:T(4,128)}, u32[]{:S(2)}) copy-start(f32[6,4,512]{2,1,0:T(4,128)} %bg_ref.9) | copy-start | bytes 147460
  0.6 3.8 %copy-start = (bf16[6,512,512]{2,1,0:T(8,128)(2,1)S(1)}, bf16[6,512,512]{2,1,0:T(8,128)(2,1)}, u32[]{:S(2)}) copy-start(bf16[6,512,512]{2,1,0:T(8,128)(2,1)} %w5_ref.1) | copy-start | bytes 9437188
  0.7 3.7 %copy-start.3 = (bf16[16,16,16,474]{3,2,1,0:T(8,128)(2,1)S(1)}, bf16[16,16,16,474]{3,2,1,0:T(8,128)(2,1)}, u32[]{:S(2)}) copy-start(bf16[16,16,16,474]{3,2,1,0:T(8,128)(2,1)} %x_ref.1) | copy-start | bytes 11649028
  0.7 0.8 %copy-start.7 = (bf16[8,48,4]{1,2,0:T(4,128)(2,1)S(1)}, bf16[8,48,4]{1,2,0:T(4,128)(2,1)}, u32[]{:S(2)}) copy-start(bf16[8,48,4]{1,2,0:T(4,128)(2,1)} %param.15) | copy-start | bytes 9220
  1.5 1.1 %copy-start.8 = (s32[8,48]{1,0:T(8,128)S(1)}, s32[8,48]{1,0:T(8,128)}, u32[]{:S(2)}) copy-start(s32[8,48]{1,0:T(8,128)} %send_ref.1) | copy-start | bytes 4612
  2.6 0.9 %copy-start.9 = (s32[8,48]{1,0:T(8,128)S(1)}, s32[8,48]{1,0:T(8,128)}, u32[]{:S(2)}) copy-start(s32[8,48]{1,0:T(8,128)} %mask_ref.1) | copy-start | bytes 4612
  3.5 0.7 %copy-start.12 = (bf16[8,3]{0,1:T(4,128)(2,1)S(1)}, bf16[8,3]{0,1:T(4,128)(2,1)}, u32[]{:S(2)}) copy-start(bf16[8,3]{0,1:T(4,128)(2,1)} %param.14) | copy-start | bytes 148
  4.4 1.0 %copy-start.6 = (bf16[474,512]{1,0:T(8,128)(2,1)S(1)}, bf16[474,512]{1,0:T(8,128)(2,1)}, u32[]{:S(2)}) copy-start(bf16[474,512]{1,0:T(8,128)(2,1)} %wg_ref.1) | copy-start | bytes 1456132
  5.4 11.5 %copy-start.4 = (bf16[1536,512]{1,0:T(8,128)(2,1)S(1)}, bf16[1536,512]{1,0:T(8,128)(2,1)}, u32[]{:S(2)}) copy-start(bf16[1536,512]{1,0:T(8,128)(2,1)} %wmsg_ref.3) | copy-start | bytes 4718596
  5.4 11.5 %copy-start.10 = (bf16[4,512]{1,0:T(4,128)(2,1)S(1)}, bf16[4,512]{1,0:T(4,128)(2,1)}, u32[]{:S(2)}) copy-start(bf16[4,512]{1,0:T(4,128)(2,1)} %we_ref.1) | copy-start | bytes 12292
  5.4 11.5 %copy-start.11 = (bf16[3,512]{1,0:T(4,128)(2,1)S(1)}, bf16[3,512]{1,0:T(4,128)(2,1)}, u32[]{:S(2)}) copy-start(bf16[3,512]{1,0:T(4,128)(2,1)} %wm_ref.1) | copy-start | bytes 9220
  27.7 20.8 %collective-permute-start = (f32[8,16,512]{2,1,0:T(8,128)S(1)}, f32[8,16,512]{2,1,0:T(8,128)S(1)}, u32[]{:S(2)}, u32[]{:S(2)}) collective-permute-start(f32[8,16,512]{2,1,0:T(8,128)S(1)} %get-tuple-element.17), channel_id=1, source_target_pairs={{0,8},{4,12},{8,0},{12,4},{3,11},{7,15},{11,3},{15,7},{16,24},{20,... | collective-permute-start | bytes 786440 | tf_op jit(solution)/shard_map/ppermute | solution.py:533
  30.8 17.6 %collective-permute-start.1 = (f32[8,16,512]{2,1,0:T(8,128)S(1)}, f32[8,16,512]{2,1,0:T(8,128)S(1)}, u32[]{:S(2)}, u32[]{:S(2)}) collective-permute-start(f32[8,16,512]{2,1,0:T(8,128)S(1)} %get-tuple-element.18), channel_id=1, source_target_pairs={{0,4},{4,8},{8,12},{12,0},{1,5},{5,9},{9,13},{13,1},{2,6},{6,10},{... | collective-permute-start | bytes 786440 | tf_op jit(solution)/shard_map/ppermute | solution.py:533
  32.5 16.0 %collective-permute-start.2 = (f32[8,16,512]{2,1,0:T(8,128)S(1)}, f32[8,16,512]{2,1,0:T(8,128)S(1)}, u32[]{:S(2)}, u32[]{:S(2)}) collective-permute-start(f32[8,16,512]{2,1,0:T(8,128)S(1)} %get-tuple-element.19), channel_id=1, source_target_pairs={{0,12},{4,0},{8,4},{12,8},{1,13},{5,1},{9,5},{13,9},{2,14},{6,2},{... | collective-permute-start | bytes 786440 | tf_op jit(solution)/shard_map/ppermute | solution.py:533
  34.7 5.8 %copy-start.5 = (bf16[512,512]{1,0:T(8,128)(2,1)S(1)}, bf16[512,512]{1,0:T(8,128)(2,1)}, u32[]{:S(2)}) copy-start(bf16[512,512]{1,0:T(8,128)(2,1)} %wu_ref.1) | copy-start | bytes 1572868
  40.5 8.0 %copy-start.1 = (bf16[1024,512]{1,0:T(8,128)(2,1)S(1)}, bf16[1024,512]{1,0:T(8,128)(2,1)}, u32[]{:S(2)}) copy-start(bf16[1024,512]{1,0:T(8,128)(2,1)} %wn_ref.1) | copy-start | bytes 3145732
